TPU v7x, 256 devices: a whole 4x4x8 slice. The times are simulated.
256 devices in a mesh: grid: 32 (over y, x, core), rows: 8 (over z).
Axes of the slice: x: 4, y: 4, z: 8, core: 2. Of those that a mesh axis runs over, the one named last changes fastest.
Arguments:
- density: bfloat16 [32, 128, 4096], P(None, 'rows', 'grid'), as said below
- basis_values: bfloat16 [64, 16, 128, 512], P('grid', None, 'rows'), may hold values from -0.59765625 to 0.59765625
- grid_points: float32 [64, 3, 512], P('grid'), may hold values from -4 to 4
- grid_weights: float32 [64, 512], P('grid'), may hold values from 0.05 to 1
- screened_blocks: int32 [64, 16], P('grid'), may hold values from 0 to 31, as said below
Outputs:
- exchange: float32 [32, 128, 4096], P(None, 'rows', 'grid')
Inputs may be any that keep to these rules, and one draw needn't show every extreme that they name: density is symmetric: density[a, i, b * 128 + j] equals density[b, j, a * 128 + i]. `screened_blocks`: each row holds 16 distinct block numbers.
All inputs are finite; a program needn't handle non-finite values.
Results may differ from a plain program's by a relative error of at most 0.00055.
The roundings to bfloat16 on the way count: a program that leaves them out, or rounds other values in their place, can miss the bound.
Values may be sent and summed in bfloat16 or wider, within the bound.
A program may use at most 64 MiB of HBM per device.

v0:
```python
import jax
import jax.numpy as jnp
from jax import lax
from jax.sharding import PartitionSpec as P


def copy_for_each(shard, axis):
    copies = jnp.broadcast_to(shard, (lax.axis_size(axis), *shard.shape))
    return lax.all_to_all(copies, axis, split_axis=0, concat_axis=0, tiled=True)


def joined_along(blocks, dim):
    shape = list(blocks.shape[1:])
    shape[dim] *= blocks.shape[0]
    return jnp.moveaxis(blocks, 0, dim).reshape(shape)


def gather_directly(shard, axis, dim):
    blocks = copy_for_each(shard, axis)
    return joined_along(blocks, dim)


def body(density, basis_values, grid_points, grid_weights, screened_blocks):
    nblocks = density.shape[0]
    rows_mine = density.shape[1]
    block_size = rows_mine * lax.axis_size("rows")
    nbasis = nblocks * block_size
    nsig = basis_values.shape[1]
    npoints = basis_values.shape[3]
    stripe = lax.all_gather(density, "grid", axis=2, tiled=True)
    totals = jnp.zeros((nblocks, rows_mine, nblocks, block_size), jnp.float32)
    for batch_index in range(basis_values.shape[0]):
        blocks = screened_blocks[batch_index]
        row_pick = jnp.take(stripe, blocks, axis=0).reshape(nsig * rows_mine, nblocks, block_size)
        chosen = jnp.take(row_pick, blocks, axis=1)
        local_values = basis_values[batch_index]
        x_mine = local_values.reshape(nsig * rows_mine, npoints)
        fsum = jnp.einsum(
            "mtk,tkp->mp",
            chosen,
            gather_directly(local_values, "rows", 1),
            preferred_element_type=jnp.float32,
        )
        fmat = fsum.astype(jnp.bfloat16)
        intersection_part = lax.dot_general(
            x_mine, fmat, (((0,), (0,)), ((), ())), preferred_element_type=jnp.float32
        )
        intersection = lax.psum(intersection_part, "rows")
        places = grid_points[batch_index]
        weights = grid_weights[batch_index]
        diffs = places[:, :, None] - places[:, None, :]
        kern = 1.0 / jnp.sqrt(jnp.sum(diffs * diffs, axis=0) + 0.5)
        mixed = (weights[:, None] * kern * intersection).astype(jnp.bfloat16)
        potential = (
            jnp.dot(x_mine, mixed, preferred_element_type=jnp.float32) * weights[None, :]
        ).astype(jnp.bfloat16)
        potential = potential.reshape(nsig, rows_mine, npoints)
        block_k = jnp.einsum(
            "mp,tkp->mtk",
            x_mine,
            lax.all_gather(potential, "rows", axis=1, tiled=True),
            preferred_element_type=jnp.float32,
        )
        block_k = block_k.reshape(nsig, rows_mine, nsig, block_size)
        totals = totals.at[blocks[:, None], :, blocks[None, :], :].add(
            block_k.transpose(0, 2, 1, 3)
        )
    return lax.psum_scatter(
        totals.reshape(nblocks, rows_mine, nbasis), "grid", scatter_dimension=2, tiled=True
    )


def solution(mesh):
    placed = (
        P(None, "rows", "grid"),
        P("grid", None, "rows", None),
        P("grid", None, None),
        P("grid", None),
        P("grid", None),
    )
    return jax.shard_map(
        body, mesh=mesh, in_specs=placed, out_specs=P(None, "rows", "grid"), check_vma=False
    )
```

profile of v0, /device:TPU:2, one launch (start us, length us, event | category | flops | bytes accessed | tf_op | source)
XLA Modules:
  0.0 494.6 jit_solution(1196830963108560420)
XLA Ops:
  6.5 0.7 all-gather.4.cloned.1.call-update
  7.3 1.1 slice_bitcast_fusion
  8.4 0.3 broadcast_in_dim.59
  8.6 59.6 %all_to_all.10 = bf16[8,16,16,512]{3,2,1,0:T(8,128)(2,1)} all-to-all(bf16[8,16,16,512]{3,2,1,0:T(8,128)(2,1)S(1)} %broadcast_in_dim.59), channel_id=1, replica_groups=mesh['grid'=32,'rows'=8] {'rows'}, dimensions={0} | all-to-all | bytes 4194304 | tf_op jit(solution)/shard_map/all_to_all | solution.py:9
  68.2 1.6 broadcast_in_dim.55
  69.8 3.7 all-to-all-start
  73.5 0.0 all-reduce.3.cloned.1.call-start
  73.7 3.2 copy.34
  76.8 46.5 %all-to-all-done = bf16[8,16,16,512]{3,2,1,0:T(8,128)(2,1)S(1)} async-done(((bf16[8,16,16,512]{3,2,1,0:T(8,128)(2,1)}), bf16[8,16,16,512]{3,2,1,0:T(8,128)(2,1)S(1)}, u32[]{:S(2)}, u32[]{:S(2)}) %all-to-all-start) | async-done | bytes 2097184 | tf_op jit(solution)/shard_map/all_to_all | solution.py:9
  123.3 1.6 copy.29
  124.9 2.9 gather_fusion.2
  127.8 0.3 broadcast_select_fusion
  128.0 0.5 copy.42
  128.5 0.8 copy.33
  129.3 1.7 gather_fusion.3
  131.1 2.9 gather_fusion
  134.0 0.3 broadcast_select_fusion.1
  134.2 0.5 copy.41
  134.7 0.8 copy.28
  135.5 1.7 gather_fusion.1
  137.2 4.1 convolution_bitcast_fusion.2
  141.3 3.3 convolution_bitcast_fusion.3
  144.6 0.6 copy-done.1
  145.3 0.4 multiply_reduce_fusion.1
  145.7 0.3 copy.27
  146.0 77.3 %all-reduce.3.cloned.1.call-done = (f32[512,512]{0,1:T(8,128)}, f32[512,512]{0,1:T(8,128)}) async-done(((f32[512,512]{0,1:T(8,128)}, f32[512,512]{0,1:T(8,128)}), (f32[512,512]{0,1:T(8,128)}, f32[512,512]{0,1:T(8,128)})) %all-reduce.3.cloned.1.call-update) | async-done | bytes 2097168 | tf_op jit(solution)/shard_map/psum | solution.py:48
  223.3 2.3 fusion
  225.7 0.0 all-gather.8.cloned.1.call-start
  225.7 0.4 multiply_reduce_fusion
  226.1 0.3 copy.32
  226.4 2.3 fusion.1
  228.7 0.2 reduce-scatter.2.cloned.1.call-start
  229.0 0.1 or_select_fusion
  229.1 0.1 reshape.140
  229.2 0.1 reshape.146
  229.3 36.4 %all-gather.6.cloned.1.call-done = bf16[16,128,512]{2,1,0:T(8,128)(2,1)} async-done(((bf16[16,16,512]{2,1,0:T(8,128)(2,1)}), bf16[16,128,512]{2,1,0:T(8,128)(2,1)}) %all-gather.6.cloned.1.call-update) | async-done | bytes 2097168 | tf_op jit(solution)/shard_map/all_gather | solution.py:61
  265.7 2.3 convolution_bitcast_fusion.1
  268.0 2.0 copy.30
  270.0 2.3 copy.31
  272.2 34.5 %all-gather.8.cloned.1.call-done = bf16[16,128,512]{2,1,0:T(8,128)(2,1)} async-done(((bf16[16,16,512]{2,1,0:T(8,128)(2,1)}), bf16[16,128,512]{2,1,0:T(8,128)(2,1)}) %all-gather.8.cloned.1.call-update) | async-done | bytes 2097168 | tf_op jit(solution)/shard_map/all_gather | solution.py:61
  306.8 3.6 convolution_bitcast_fusion
  310.4 3.1 copy.35
  313.5 3.6 copy.36
  317.1 4.2 broadcast_in_dim.51
  321.3 28.4 %scatter_fusion = f32[32,16,32,128]{3,1,2,0:T(8,128)} fusion(f32[32,16,32,128]{3,1,2,0:T(8,128)} %broadcast_in_dim.51, s32[256]{0:T(256)S(1)} %reshape.140, f32[256,16,128]{2,1,0:T(8,128)S(1)} %bitcast.107), kind=kCustom, calls=%fused_computation.4 | custom fusion | flops 524288 | bytes 6293504 | tf_op jit(solution)/shard_map/scatter-add | solution.py:65
  349.7 31.8 %scatter_fusion.1 = f32[32,16,32,128]{3,1,2,0:T(8,128)} fusion(f32[32,16,32,128]{3,1,2,0:T(8,128)} %scatter_fusion, s32[256]{0:T(256)S(1)} %reshape.146, f32[256,16,128]{2,1,0:T(8,128)} %bitcast.108), kind=kCustom, calls=%fused_computation.5 | custom fusion | flops 524288 | bytes 6293504 | tf_op jit(solution)/shard_map/scatter-add | solution.py:65
  381.5 7.8 %copy_bitcast_fusion = f32[32,16,4096]{2,1,0:T(8,128)} fusion(f32[32,16,32,128]{3,1,2,0:T(8,128)} %scatter_fusion.1), kind=kLoop, calls=%fused_computation.6 | loop fusion | bytes 16777216 | tf_op jit(solution)/shard_map/reshape | solution.py:69
  389.3 98.8 %reduce-scatter.2.cloned.1.call-done = f32[32,16,128]{2,1,0:T(8,128)} async-done(((f32[32,16,4096]{2,1,0:T(8,128)}), f32[32,16,128]{2,1,0:T(8,128)}) %reduce-scatter.2.cloned.1.call-update) | async-done | bytes 262160 | tf_op jit(solution)/shard_map/reduce_scatter | solution.py:68
  (25 shorter events, 0.2 us)
Async XLA Ops:
  6.5 118.4 %all-gather.4.cloned.1.call-start = ((), (), s32[]{:S(2)}) async-start(), calls=%async_computation.3 | async-start | bytes 4325376 | tf_op jit(solution)/shard_map/all_gather | solution.py:30
  69.8 3.8 copy-start.3
  69.8 53.5 %all-to-all-start = ((bf16[8,16,16,512]{3,2,1,0:T(8,128)(2,1)}), bf16[8,16,16,512]{3,2,1,0:T(8,128)(2,1)S(1)}, u32[]{:S(2)}, u32[]{:S(2)}) async-start(bf16[8,16,16,512]{3,2,1,0:T(8,128)(2,1)} %broadcast_in_dim.55), calls=%async_computation | async-start | bytes 4194304 | tf_op jit(solution)/shard_map/all_to_all | solution.py:9
  73.5 149.8 %all-reduce.3.cloned.1.call-start = ((), (), s32[]{:S(2)}) async-start(), calls=%async_computation.7 | async-start | bytes 4194304 | tf_op jit(solution)/shard_map/psum | solution.py:48
  137.2 4.1 copy-start
  144.6 0.7 copy-start.1
  144.6 1.4 copy-start.2
  144.6 121.1 %all-gather.6.cloned.1.call-start = ((), (), s32[]{:S(2)}) async-start(), calls=%async_computation.4 | async-start | bytes 2359296 | tf_op jit(solution)/shard_map/all_gather | solution.py:61
  225.7 81.1 %all-gather.8.cloned.1.call-start = ((), (), s32[]{:S(2)}) async-start(), calls=%async_computation.5 | async-start | bytes 2359296 | tf_op jit(solution)/shard_map/all_gather | solution.py:61
  228.7 259.3 %reduce-scatter.2.cloned.1.call-start = ((), (), s32[]{:S(2)}) async-start(), calls=%async_computation.6 | async-start | bytes 8650752 | tf_op jit(solution)/shard_map/reduce_scatter | solution.py:68
Sparse Core Ops, SparseCore 0:
  9.8 56.2 all-gather.3
  144.7 78.5 all-reduce.2
  225.8 39.8 all-gather.5
  267.3 39.4 all-gather.7
  389.4 98.5 reduce-scatter.1
where the time goes:
time: 496 us; the launch traced here: 495 us
  waiting for transfers between devices  294 us (59%)
  other arithmetic  61.6 us (12%)
  blocking collectives  59.6 us (12%)
  local copies, waits for them, and re-layouts  43.8 us (9%)
  matrix products  17.9 us (4%)
  between operations  13.4 us (3%)
    reduce_scatter x1, waiting for transfers between devices, body(): lax.psum_scatter(totals.reshape(nblocks, rows_mine, nbasis), 'grid', scat...  98.8 us
    psum x1, waiting for transfers between devices, body(): intersection = lax.psum(intersection_part, 'rows')  77.3 us
    all_gather x2, waiting for transfers between devices, body(): lax.all_gather(potential, 'rows', axis=1, tiled=True)  70.9 us
    scatter-add x2, other arithmetic, body(): totals.at[blocks[:, None], :, blocks[None, :], :]  60.2 us
    all_to_all x1, blocking collectives, copy_for_each(): return lax.all_to_all(copies, axis, split_axis=0, concat_axis=0, tiled=True)  59.6 us
    all_to_all x1, waiting for transfers between devices, copy_for_each(): return lax.all_to_all(copies, axis, split_axis=0, concat_axis=0, tiled=True)  46.5 us
  transfers between devices with their start and end apart: 6, of which 5 were waited for; matrix products, arithmetic and copies ran while one was open for 4% of the time, Pallas kernels for 0%

commit v1 on v0

--- a/solution.py
+++ b/solution.py
@@ -58,7 +58,9 @@
         block_k = jnp.einsum(
             "mp,tkp->mtk",
             x_mine,
-            lax.all_gather(potential, "rows", axis=1, tiled=True),
+            jnp.concatenate(
+                lax.all_to_all(jnp.stack([potential] * lax.axis_size("rows")), "rows", 0, 0), axis=1
+            ),
             preferred_element_type=jnp.float32,
         )
         block_k = block_k.reshape(nsig, rows_mine, nsig, block_size)

time: 496 us -> 520 us (1.048)
  waiting for transfers between devices: 294 us -> 304 us
  starting transfers between devices: 4.08 us -> 13 us
  local copies, waits for them, and re-layouts: 43.8 us -> 52 us
    all_to_all x0 -> x2, waiting for transfers between devices: none -> 82.8 us  [body(): lax.all_to_all(jnp.stack([potential] * lax.axis_size('rows')), 'rows', 0, 0)]
    all_gather x2 -> x0, waiting for transfers between devices: 70.9 us -> none  [body(): lax.all_gather(potential, 'rows', axis=1, tiled=True)]
    all_to_all x0 -> x2, starting transfers between devices: none -> 9.02 us  [body(): lax.all_to_all(jnp.stack([potential] * lax.axis_size('rows')), 'rows', 0, 0)]
where the time goes in v1:
time: 520 us; the launch traced here: 518 us
  waiting for transfers between devices  304 us (58%)
  other arithmetic  62.6 us (12%)
  blocking collectives  59.6 us (11%)
  local copies, waits for them, and re-layouts  52 us (10%)
  matrix products  14.1 us (3%)
  between operations  13.4 us (3%)
  starting transfers between devices  13 us (2%)
    reduce_scatter x1, waiting for transfers between devices, body(): lax.psum_scatter(totals.reshape(nblocks, rows_mine, nbasis), 'grid', scat...  96.4 us
    all_to_all x2, waiting for transfers between devices, body(): lax.all_to_all(jnp.stack([potential] * lax.axis_size('rows')), 'rows', 0, 0)  82.8 us
    psum x1, waiting for transfers between devices, body(): intersection = lax.psum(intersection_part, 'rows')  77.3 us
    scatter-add x2, other arithmetic, body(): totals.at[blocks[:, None], :, blocks[None, :], :]  60.2 us
    all_to_all x1, blocking collectives, copy_for_each(): return lax.all_to_all(copies, axis, split_axis=0, concat_axis=0, tiled=True)  59.6 us
    all_to_all x1, waiting for transfers between devices, copy_for_each(): return lax.all_to_all(copies, axis, split_axis=0, concat_axis=0, tiled=True)  46.5 us
  transfers between devices with their start and end apart: 6, of which 5 were waited for; matrix products, arithmetic and copies ran while one was open for 4% of the time, Pallas kernels for 0%

profile of v1, /device:TPU:2, one launch (start us, length us, event | category | flops | bytes accessed | tf_op | source)
XLA Modules:
  0.0 518.3 jit_solution(15890061425346790377)
XLA Ops:
  6.5 0.7 all-gather.2.cloned.1.call-update
  7.3 1.2 slice_bitcast_fusion
  8.4 0.3 broadcast_in_dim.59
  8.7 59.6 %all_to_all.20 = bf16[8,16,16,512]{3,2,1,0:T(8,128)(2,1)} all-to-all(bf16[8,16,16,512]{3,2,1,0:T(8,128)(2,1)S(1)} %broadcast_in_dim.59), channel_id=1, replica_groups=mesh['grid'=32,'rows'=8] {'rows'}, dimensions={0} | all-to-all | bytes 4194304 | tf_op jit(solution)/shard_map/all_to_all | solution.py:9
  68.3 1.6 broadcast_in_dim.55
  69.9 3.7 all-to-all-start
  73.7 3.2 copy.37
  76.9 46.5 %all-to-all-done = bf16[8,16,16,512]{3,2,1,0:T(8,128)(2,1)S(1)} async-done(((bf16[8,16,16,512]{3,2,1,0:T(8,128)(2,1)}), bf16[8,16,16,512]{3,2,1,0:T(8,128)(2,1)S(1)}, u32[]{:S(2)}, u32[]{:S(2)}) %all-to-all-start) | async-done | bytes 2097184 | tf_op jit(solution)/shard_map/all_to_all | solution.py:9
  123.4 1.6 copy.31
  125.0 2.9 gather_fusion.2
  127.8 0.3 broadcast_select_fusion
  128.1 0.5 copy.46
  128.6 0.8 copy.36
  129.4 1.7 gather_fusion.3
  131.2 2.9 gather_fusion
  134.0 0.3 broadcast_select_fusion.1
  134.3 0.5 copy.45
  134.8 0.8 copy.30
  135.6 1.7 gather_fusion.1
  137.3 4.1 convolution_bitcast_fusion.2
  141.4 3.3 convolution_bitcast_fusion.3
  144.7 0.7 copy-done.3
  145.4 0.4 multiply_reduce_fusion.1
  145.8 0.3 copy.29
  146.1 77.3 %all-reduce.3.cloned.1.call-done = (f32[512,512]{0,1:T(8,128)}, f32[512,512]{0,1:T(8,128)}) async-done(((f32[512,512]{0,1:T(8,128)}, f32[512,512]{0,1:T(8,128)}), (f32[512,512]{0,1:T(8,128)}, f32[512,512]{0,1:T(8,128)})) %all-reduce.3.cloned.1.call-update) | async-done | bytes 2097168 | tf_op jit(solution)/shard_map/psum | solution.py:48
  223.5 1.6 fusion
  225.1 1.6 stack.6
  226.7 4.7 all-to-all-start.1
  231.4 1.4 multiply_reduce_fusion
  232.7 1.6 copy.35
  234.3 2.3 fusion.1
  236.6 41.6 %all-to-all-done.1 = bf16[8,16,16,512]{3,2,1,0:T(8,128)(2,1)S(1)} async-done(((bf16[8,16,16,512]{3,2,1,0:T(8,128)(2,1)}), bf16[8,16,16,512]{3,2,1,0:T(8,128)(2,1)S(1)}, u32[]{:S(2)}, u32[]{:S(2)}) %all-to-all-start.1) | async-done | bytes 2097184 | tf_op jit(solution)/shard_map/all_to_all | solution.py:62
  278.2 2.5 stack.7
  280.8 4.3 all-to-all-start.3
  285.9 0.7 copy-done.1
  286.6 0.7 convolution_bitcast_fusion.1
  287.3 2.0 copy.33
  289.3 2.3 copy.34
  291.6 41.2 %all-to-all-done.3 = bf16[8,16,16,512]{3,2,1,0:T(8,128)(2,1)} async-done(((bf16[8,16,16,512]{3,2,1,0:T(8,128)(2,1)}), bf16[8,16,16,512]{3,2,1,0:T(8,128)(2,1)}, u32[]{:S(2)}, u32[]{:S(2)}) %all-to-all-start.3) | async-done | bytes 2097184 | tf_op jit(solution)/shard_map/all_to_all | solution.py:62
  332.7 1.8 copy.38
  334.5 2.1 convolution_bitcast_fusion
  336.6 3.1 copy.39
  339.7 3.6 copy.40
  343.3 4.2 broadcast_in_dim.51
  347.5 28.4 %scatter_fusion = f32[32,16,32,128]{3,1,2,0:T(8,128)} fusion(f32[32,16,32,128]{3,1,2,0:T(8,128)} %broadcast_in_dim.51, s32[256]{0:T(256)S(1)} %reshape.152, f32[256,16,128]{2,1,0:T(8,128)S(1)} %bitcast.111), kind=kCustom, calls=%fused_computation.4 | custom fusion | flops 524288 | bytes 6293504 | tf_op jit(solution)/shard_map/scatter-add | solution.py:67
  375.9 31.8 %scatter_fusion.1 = f32[32,16,32,128]{3,1,2,0:T(8,128)} fusion(f32[32,16,32,128]{3,1,2,0:T(8,128)} %scatter_fusion, s32[256]{0:T(256)S(1)} %reshape.158, f32[256,16,128]{2,1,0:T(8,128)} %bitcast.112), kind=kCustom, calls=%fused_computation.5 | custom fusion | flops 524288 | bytes 6293504 | tf_op jit(solution)/shard_map/scatter-add | solution.py:67
  407.7 7.8 %copy_bitcast_fusion = f32[32,16,4096]{2,1,0:T(8,128)} fusion(f32[32,16,32,128]{3,1,2,0:T(8,128)} %scatter_fusion.1), kind=kLoop, calls=%fused_computation.6 | loop fusion | bytes 16777216 | tf_op jit(solution)/shard_map/reshape | solution.py:71
  415.4 96.4 %reduce-scatter.2.cloned.1.call-done = f32[32,16,128]{2,1,0:T(8,128)} async-done(((f32[32,16,4096]{2,1,0:T(8,128)}), f32[32,16,128]{2,1,0:T(8,128)}) %reduce-scatter.2.cloned.1.call-update) | async-done | bytes 262160 | tf_op jit(solution)/shard_map/reduce_scatter | solution.py:70
  (31 shorter events, 0.8 us)
Async XLA Ops:
  6.5 118.4 %all-gather.2.cloned.1.call-start = ((), (), s32[]{:S(2)}) async-start(), calls=%async_computation.5 | async-start | bytes 4325376 | tf_op jit(solution)/shard_map/all_gather | solution.py:30
  8.4 215.1 %copy-start = (bf16[1,16,16,512]{3,2,1,0:T(8,128)(2,1)}, bf16[1,16,16,512]{3,2,1,0:T(8,128)(2,1)S(1)}, u32[]{:S(2)}) copy-start(bf16[1,16,16,512]{3,2,1,0:T(8,128)(2,1)S(1)} %get-tuple-element.16) | copy-start | bytes 786436
  69.9 3.8 copy-start.5
  69.9 53.5 %all-to-all-start = ((bf16[8,16,16,512]{3,2,1,0:T(8,128)(2,1)}), bf16[8,16,16,512]{3,2,1,0:T(8,128)(2,1)S(1)}, u32[]{:S(2)}, u32[]{:S(2)}) async-start(bf16[8,16,16,512]{3,2,1,0:T(8,128)(2,1)} %broadcast_in_dim.55), calls=%async_computation | async-start | bytes 4194304 | tf_op jit(solution)/shard_map/all_to_all | solution.py:9
  73.6 149.9 %all-reduce.3.cloned.1.call-start = ((), (), s32[]{:S(2)}) async-start(), calls=%async_computation.7 | async-start | bytes 4194304 | tf_op jit(solution)/shard_map/psum | solution.py:48
  137.3 4.1 copy-start.2
  144.7 0.7 copy-start.3
  145.4 0.7 copy-start.4
  226.7 51.6 %all-to-all-start.1 = ((bf16[8,16,16,512]{3,2,1,0:T(8,128)(2,1)}), bf16[8,16,16,512]{3,2,1,0:T(8,128)(2,1)S(1)}, u32[]{:S(2)}, u32[]{:S(2)}) async-start(bf16[8,16,16,512]{3,2,1,0:T(8,128)(2,1)} %stack.6), calls=%async_computation.1 | async-start | bytes 4194304 | tf_op jit(solution)/shard_map/all_to_all | solution.py:62
  280.8 52.0 %all-to-all-start.3 = ((bf16[8,16,16,512]{3,2,1,0:T(8,128)(2,1)}), bf16[8,16,16,512]{3,2,1,0:T(8,128)(2,1)}, u32[]{:S(2)}, u32[]{:S(2)}) async-start(bf16[8,16,16,512]{3,2,1,0:T(8,128)(2,1)} %stack.7), calls=%async_computation.3 | async-start | bytes 4194304 | tf_op jit(solution)/shard_map/all_to_all | solution.py:62
  285.1 226.7 %reduce-scatter.2.cloned.1.call-start = ((), (), s32[]{:S(2)}) async-start(), calls=%async_computation.6 | async-start | bytes 8650752 | tf_op jit(solution)/shard_map/reduce_scatter | solution.py:70
  285.6 1.0 copy-start.1
Sparse Core Ops, SparseCore 0:
  9.8 56.2 all-gather.1
  144.8 78.6 all-reduce.2
  415.6 96.1 reduce-scatter.1
